TPU v7x, 32 devices: a whole 2x2x4 slice. The times are simulated.
32 devices in a mesh: ga: 8 (over z, x), band: 4 (over y, core).
Axes of the slice: x: 2, y: 2, z: 4, core: 2. Of those that a mesh axis runs over, the one named last changes fastest.
Arguments:
- coeffs: bfloat16 [2, 512, 40960], P(None, ('ga', 'band')), may hold values from -6 to 6
- projectors: bfloat16 [1280, 2, 40960], P(None, None, 'ga'), may hold values from -0.01953125 to 0.01953125
- block_coupling: float32 [1280, 18], replicated, may hold values from -12 to 12
- atom_counts: int32 [160], replicated, may hold values from 4 to 18, as said below
- wave_counts: int32 [8], P('ga'), may hold values from 3840 to 5120
Outputs:
- applied: bfloat16 [2, 512, 40960], P(None, ('ga', 'band'))
- band_energy: float32 [512], P(('ga', 'band'))
- total_energy: float32 [], replicated
Inputs may be any that keep to these rules, and one draw needn't show every extreme that they name: `atom_counts`: each atom has 4, 8 or 18 projectors, the counts sum to 1280 and the largest is 18.
All inputs are finite; a program needn't handle non-finite values.
Results may differ from a plain program's by a relative error of at most 0.013.
Values may be sent and summed in bfloat16 or wider, within the bound.
A program may use at most 128 MiB of HBM per device.

v0:
```python
import math
import jax
import jax.numpy as jnp
from jax import lax
from jax.sharding import PartitionSpec as P


def block_tables(atom_counts, row_ids):
    atom_ends = jnp.cumsum(atom_counts)
    atom_starts = atom_ends - atom_counts
    inside = (atom_starts[None, :] <= row_ids[:, None]) & (atom_ends[None, :] > row_ids[:, None])
    block_first = jnp.sum(jnp.where(inside, atom_starts[None, :], 0), axis=1)
    block_length = jnp.sum(jnp.where(inside, atom_counts[None, :], 0), axis=1)
    return (block_first, block_length)


def coupling_matrix(block_first, block_length, coupling_rows, column_count):
    column_ids = lax.iota(jnp.int32, column_count)
    offsets = column_ids[None, :] - block_first[:, None]
    matrix = jnp.zeros((coupling_rows.shape[0], column_count), jnp.float32)
    for offset in range(coupling_rows.shape[1]):
        hit = (offsets == offset) & (offset < block_length[:, None])
        matrix = jnp.where(hit, coupling_rows[:, offset : offset + 1], matrix)
    return matrix


def shards(coeffs, projectors, block_coupling, atom_counts, wave_counts):
    moved_bands = lax.all_to_all(coeffs, "ga", split_axis=2, concat_axis=1, tiled=True)
    own_bands = coeffs.shape[1]
    group_bands = moved_bands.shape[1]
    wave_slots = projectors.shape[2]
    proj_total_rows = projectors.shape[0]
    in_sphere = (lax.iota(jnp.int32, wave_slots) < wave_counts[0]).astype(jnp.float32)
    masked = moved_bands * in_sphere.astype(jnp.bfloat16)
    real_part = masked[0]
    imag_part = masked[1]
    stacked = jnp.concatenate(
        [jnp.concatenate([real_part, imag_part], 1), jnp.concatenate([imag_part, -real_part], 1)], 0
    )
    flat_beta = projectors.reshape(proj_total_rows, 2 * wave_slots)
    contract_last = (((1,), (1,)), ((), ()))
    contract_first = (((0,), (0,)), ((), ()))
    ga_index = lax.axis_index("ga")
    local_terms = lax.dot_general(
        flat_beta, stacked, contract_last, preferred_element_type=jnp.float32
    )
    projections = lax.psum(local_terms, "ga")
    block_first, block_length = block_tables(atom_counts, lax.iota(jnp.int32, proj_total_rows))
    matrix = coupling_matrix(block_first, block_length, block_coupling, proj_total_rows)
    coupled = jnp.dot(
        matrix, projections, precision=lax.Precision.HIGHEST, preferred_element_type=jnp.float32
    )
    energy_terms = jnp.sum(projections * coupled, axis=0)
    group_energy = (energy_terms[:group_bands] + energy_terms[group_bands:]) / proj_total_rows
    band_energy = lax.dynamic_slice_in_dim(group_energy, ga_index * own_bands, own_bands, 0)
    total_energy = lax.psum(jnp.sum(group_energy), "band")
    products = lax.dot_general(
        coupled.astype(jnp.bfloat16), flat_beta, contract_first, preferred_element_type=jnp.float32
    )
    band_total = own_bands * lax.axis_size("ga") * lax.axis_size("band")
    total_energy = total_energy / math.sqrt(band_total)
    real_out = products[:group_bands, :wave_slots] - products[group_bands:, wave_slots:]
    imag_out = products[:group_bands, wave_slots:] + products[group_bands:, :wave_slots]
    result = (jnp.stack([real_out, imag_out]) * in_sphere).astype(jnp.bfloat16)
    applied = lax.all_to_all(result, "ga", split_axis=1, concat_axis=2, tiled=True)
    return (applied, band_energy, total_energy)


def solution(mesh):
    placed = (P(None, ("ga", "band"), None), P(None, None, "ga"), P(), P(), P("ga"))
    return jax.shard_map(
        shards,
        mesh=mesh,
        in_specs=placed,
        out_specs=(P(None, ("ga", "band"), None), P(("ga", "band")), P()),
        check_vma=False,
    )
```

profile of v0, /device:TPU:0, one launch (start us, length us, event | category | flops | bytes accessed | tf_op | source)
XLA Modules:
  0.0 439.4 jit_solution(13984395675737779399)
XLA Ops:
  7.2 38.0 %copy.21 = bf16[2,16,40960]{1,0,2:T(2,128)(2,1)} copy(bf16[2,16,40960]{2,1,0:T(8,128)(2,1)} %param.5) | data formatting | bytes 5242880 | tf_op args[0]
  45.1 24.1 %reshape.129 = bf16[8,2,81920]{2,1,0:T(2,128)(2,1)} reshape(bf16[40960,2,16]{2,1,0:T(2,128)(2,1)} %bitcast.40) | data formatting | bytes 5242880
  69.2 7.3 %all-to-all-start = ((bf16[8,2,81920]{2,1,0:T(2,128)(2,1)}), bf16[8,2,81920]{2,1,0:T(2,128)(2,1)S(1)}, u32[]{:S(2)}, u32[]{:S(2)}) async-start(bf16[8,2,81920]{2,1,0:T(2,128)(2,1)} %reshape.129), calls=%async_computation | async-start | bytes 5242880 | tf_op jit(solution)/shard_map/all_to_all | solution.py:28
  76.5 0.4 all-reduce.3.cloned.1.call-start
  77.6 23.8 %copy.29 = bf16[160,8,2,5120]{3,1,2,0:T(8,128)(2,1)} copy(bf16[160,8,2,5120]{3,2,1,0:T(2,128)(2,1)} %bitcast.41) | data formatting | bytes 52428800
  101.3 34.6 %all-to-all-done = bf16[8,2,81920]{2,1,0:T(2,128)(2,1)S(1)} async-done(((bf16[8,2,81920]{2,1,0:T(2,128)(2,1)}), bf16[8,2,81920]{2,1,0:T(2,128)(2,1)S(1)}, u32[]{:S(2)}, u32[]{:S(2)}) %all-to-all-start) | async-done | bytes 2621472 | tf_op jit(solution)/shard_map/all_to_all | solution.py:28
  136.0 17.1 %reshape.130 = bf16[40960,2,16]{2,1,0:T(2,128)(2,1)} reshape(bf16[8,2,81920]{2,1,0:T(2,128)(2,1)S(1)} %all-to-all-done) | data formatting | bytes 5242880
  153.0 37.5 %copy.28 = bf16[2,16,8,5120]{3,1,2,0:T(8,128)(2,1)S(1)} copy(bf16[2,16,8,5120]{1,0,3,2:T(2,128)(2,1)} %bitcast.39) | data formatting | bytes 5242880 | tf_op jit(solution)/shard_map/all_to_all | solution.py:28
  190.5 0.3 bitcast_multiply_fusion
  190.9 0.2 slice_bitcast_fusion.1
  191.1 0.1 fusion.168
  191.2 0.0 copy-start.1
  191.2 0.0 copy-start
  191.2 28.8 %fusion.138 = f32[1280,256]{0,1:T(8,128)} fusion(bf16[1280,10240]{1,0:T(8,128)(2,1)} %bitcast.37, bf16[128,5120]{1,0:T(8,128)(2,1)S(1)} %fusion.168, bf16[128,5120]{1,0:T(8,128)(2,1)S(1)} %get-tuple-element.28, bf16[128,5120]{1,0:T(8,128)(2,1)S(1)} %get-tuple-element.27), kind=kOutput, calls=%fused_computation.122 | convolution fusion | flops 6731857920 | bytes 31457280 | tf_op jit(solution)/shard_map/dot_general | solution.py:44
  220.0 0.0 all-reduce.3.cloned.1.call-update
  220.1 0.0 copy-done.1
  220.1 0.3 reduce-window.9
  220.4 0.1 slice.88
  220.5 0.1 slice_reduce_fusion.18
  220.6 0.0 copy-done
  220.6 0.2 slice_reduce_fusion.17
  220.9 0.1 add_bitcast_fusion
  220.9 0.3 select_reduce_fusion
  221.3 81.6 %all-reduce.3.cloned.1.call-done = f32[1280,256]{0,1:T(8,128)} async-done(((f32[1280,256]{0,1:T(8,128)}), f32[1280,256]{0,1:T(8,128)}) %all-reduce.3.cloned.1.call-update) | async-done | bytes 1310736 | tf_op jit(solution)/shard_map/psum | solution.py:47
  303.0 39.1 %fusion = f32[1280,256]{1,0:T(8,128)} fusion(f32[1280,256]{0,1:T(8,128)} %all-reduce.3.cloned.1.call-done, f32[1280]{0:T(1024)S(1)} %get-tuple-element.19, f32[1280]{0:T(1024)S(1)} %get-tuple-element.20, f32[1280]{0:T(1024)S(1)} %get-tuple-element.4, f32[1280]{0:T(1024)S(1)} %get-tuple-element.5, f32[1280]{0:T(1024)S(1)} %get-tuple-element.6, ...), kind=kOutput, calls=%fused_computation | convolution fusion | flops 5123276800 | bytes 2741760 | tf_op jit(solution)/shard_map/dot_general | solution.py:50
  342.1 13.0 %fusion.144 = f32[256,10240]{1,0:T(8,128)S(1)} fusion(bf16[1280,10240]{1,0:T(8,128)(2,1)} %bitcast.38, f32[1280,256]{1,0:T(8,128)} %fusion), kind=kOutput, calls=%fused_computation.136 | convolution fusion | flops 6711214080 | bytes 38010880 | tf_op jit(solution)/shard_map/dot_general | solution.py:57
  355.1 0.8 fusion.142
  355.9 0.5 fusion.81
  356.4 4.2 copy.24
  360.6 3.7 all-to-all-start.1
  364.2 2.8 copy.26
  367.0 1.9 multiply_reduce_fusion
  368.9 0.6 fusion.169
  369.5 7.3 %psum.15 = f32[]{:T(128)} all-reduce(f32[]{:T(128)} %get-tuple-element.23), channel_id=1, replica_groups=mesh['ga'=8,'band'=4] {'band'}, use_global_device_ids=true, to_apply=%region_7.8 | all-reduce | flops 1 | bytes 8 | tf_op jit(solution)/shard_map/psum | solution.py:56
  376.9 0.6 dynamic_slice.3
  378.1 45.7 %all-to-all-done.1 = bf16[2,128,5120]{2,0,1:T(2,128)(2,1)S(1)} async-done(((bf16[2,128,5120]{2,0,1:T(2,128)(2,1)}), bf16[2,128,5120]{2,0,1:T(2,128)(2,1)S(1)}, u32[]{:S(2)}, u32[]{:S(2)}) %all-to-all-start.1) | async-done | bytes 2621472 | tf_op jit(solution)/shard_map/all_to_all | solution.py:65
  423.8 2.9 copy.25
  426.7 4.5 %all_to_all.33 = bf16[2,16,40960]{2,1,0:T(8,128)(2,1)} reshape(bf16[2,16,8,5120]{3,2,1,0:T(8,128)(2,1)} %copy.25) | data formatting | bytes 5242880 | tf_op jit(solution)/shard_map/all_to_all | solution.py:65
  (5 shorter events, 0.1 us)
Async XLA Ops:
  69.2 66.8 %all-to-all-start = ((bf16[8,2,81920]{2,1,0:T(2,128)(2,1)}), bf16[8,2,81920]{2,1,0:T(2,128)(2,1)S(1)}, u32[]{:S(2)}, u32[]{:S(2)}) async-start(bf16[8,2,81920]{2,1,0:T(2,128)(2,1)} %reshape.129), calls=%async_computation | async-start | bytes 5242880 | tf_op jit(solution)/shard_map/all_to_all | solution.py:28
  76.5 226.5 %all-reduce.3.cloned.1.call-start = ((), (), s32[]{:S(2)}) async-start(), calls=%async_computation.2 | async-start | bytes 2621440 | tf_op jit(solution)/shard_map/psum | solution.py:47
  191.2 28.9 %copy-start.1 = (s32[160]{0:T(256)S(1)}, s32[160]{0:T(256)}, u32[]{:S(2)}) copy-start(s32[160]{0:T(256)} %param.8) | copy-start | bytes 1924
  191.2 29.4 %copy-start = (f32[1280,18]{0,1:T(8,128)S(1)}, f32[1280,18]{0,1:T(8,128)}, u32[]{:S(2)}) copy-start(f32[1280,18]{0,1:T(8,128)} %param.7) | copy-start | bytes 276484
  360.6 63.2 %all-to-all-start.1 = ((bf16[2,128,5120]{2,0,1:T(2,128)(2,1)}), bf16[2,128,5120]{2,0,1:T(2,128)(2,1)S(1)}, u32[]{:S(2)}, u32[]{:S(2)}) async-start(bf16[2,128,5120]{2,0,1:T(2,128)(2,1)} %copy.24), calls=%async_computation.1 | async-start | bytes 5242880 | tf_op jit(solution)/shard_map/all_to_all | solution.py:65
Sparse Core Ops, SparseCore 0:
  220.2 82.7 all-reduce.2
where the time goes:
time: 447 us; the launch traced here: 439 us
  waiting for transfers between devices  162 us (36%)
  local copies, waits for them, and re-layouts  156 us (35%)
  matrix products  81 us (18%)
  between operations  16.8 us (4%)
  starting transfers between devices  11.4 us (3%)
  blocking collectives  7.33 us (2%)
  other arithmetic  4.94 us (1%)
    unnamed x8, local copies, waits for them, and re-layouts  103 us
    psum x1, waiting for transfers between devices, shards(): projections = lax.psum(local_terms, 'ga')  81.6 us
    all_to_all x1, waiting for transfers between devices, shards(): lax.all_to_all(result, 'ga', split_axis=1, concat_axis=2, tiled=True)  45.7 us
    dot_general x1, matrix products, shards(): jnp.dot(matrix, projections, precision=lax.Precision.HIGHEST, preferred_e...  39.1 us
    all_to_all x1, local copies, waits for them, and re-layouts, shards(): lax.all_to_all(coeffs, 'ga', split_axis=2, concat_axis=1, tiled=True)  37.5 us
    all_to_all x1, waiting for transfers between devices, shards(): lax.all_to_all(coeffs, 'ga', split_axis=2, concat_axis=1, tiled=True)  34.6 us
    dot_general x1, matrix products, shards(): lax.dot_general(flat_beta, stacked, contract_last, preferred_element_type...  28.8 us
    dot_general x1, matrix products, shards(): lax.dot_general(coupled.astype(jnp.bfloat16), flat_beta, contract_first,...  13 us
  transfers between devices with their start and end apart: 3, of which 3 were waited for; matrix products, arithmetic and copies ran while one was open for 7% of the time, Pallas kernels for 0%

commit v1 on v0

--- a/solution.py
+++ b/solution.py
@@ -3,6 +3,15 @@
 import jax.numpy as jnp
 from jax import lax
 from jax.sharding import PartitionSpec as P
+
+
+def sum_by_hops(block, axis):
+    peers = lax.axis_size(axis)
+    summed, hop = (block, 1)
+    while hop < peers:
+        summed = summed + lax.ppermute(summed, axis, [(i, i ^ hop) for i in range(peers)])
+        hop = 2 * hop
+    return summed
 
 
 def block_tables(atom_counts, row_ids):
@@ -44,7 +53,7 @@
     local_terms = lax.dot_general(
         flat_beta, stacked, contract_last, preferred_element_type=jnp.float32
     )
-    projections = lax.psum(local_terms, "ga")
+    projections = sum_by_hops(local_terms, "ga")
     block_first, block_length = block_tables(atom_counts, lax.iota(jnp.int32, proj_total_rows))
     matrix = coupling_matrix(block_first, block_length, block_coupling, proj_total_rows)
     coupled = jnp.dot(

time: 447 us -> 469 us (1.049)
  waiting for transfers between devices: 162 us -> 191 us
  between operations: 16.8 us -> 3.43 us
  starting transfers between devices: 11.4 us -> 18.2 us
    ppermute x0 -> x3, waiting for transfers between devices: none -> 111 us  [sum_by_hops(): lax.ppermute(summed, axis, [(i, i ^ hop) for i in range(peers)])]
    psum x1 -> x0, waiting for transfers between devices: 81.6 us -> none  [shards(): projections = lax.psum(local_terms, 'ga')]
    ppermute x0 -> x3, starting transfers between devices: none -> 5.68 us  [sum_by_hops(): lax.ppermute(summed, axis, [(i, i ^ hop) for i in range(peers)])]
    unnamed x8 -> x10, local copies, waits for them, and re-layouts: 103 us -> 104 us
  transfers between devices with their start and end apart: 3 -> 5, of which waited for: 3 -> 5; matrix products, arithmetic and copies ran while one was open for 7% -> 7% of each run, Pallas kernels for 0% -> 0%
where the time goes in v1:
time: 469 us; the launch traced here: 461 us
  waiting for transfers between devices  191 us (41%)
  local copies, waits for them, and re-layouts  157 us (33%)
  matrix products  78.7 us (17%)
  starting transfers between devices  18.2 us (4%)
  blocking collectives  7.41 us (2%)
  other arithmetic  5.39 us (1%)
    ppermute x3, waiting for transfers between devices, sum_by_hops(): lax.ppermute(summed, axis, [(i, i ^ hop) for i in range(peers)])  111 us
    unnamed x10, local copies, waits for them, and re-layouts  104 us
    all_to_all x1, waiting for transfers between devices, shards(): lax.all_to_all(result, 'ga', split_axis=1, concat_axis=2, tiled=True)  45.7 us
    dot_general x1, matrix products, shards(): jnp.dot(matrix, projections, precision=lax.Precision.HIGHEST, preferred_e...  37.9 us
    all_to_all x1, local copies, waits for them, and re-layouts, shards(): lax.all_to_all(coeffs, 'ga', split_axis=2, concat_axis=1, tiled=True)  37.5 us
    all_to_all x1, waiting for transfers between devices, shards(): lax.all_to_all(coeffs, 'ga', split_axis=2, concat_axis=1, tiled=True)  35 us
    dot_general x1, matrix products, shards(): lax.dot_general(flat_beta, stacked, contract_last, preferred_element_type...  27.8 us
    dot_general x1, matrix products, shards(): lax.dot_general(coupled.astype(jnp.bfloat16), flat_beta, contract_first,...  13 us
  transfers between devices with their start and end apart: 5, of which 5 were waited for; matrix products, arithmetic and copies ran while one was open for 7% of the time, Pallas kernels for 0%

profile of v1, /device:TPU:0, one launch (start us, length us, event | category | flops | bytes accessed | tf_op | source)
XLA Modules:
  0.0 461.4 jit_solution(2564692843952915864)
XLA Ops:
  0.6 38.0 %copy.21 = bf16[2,16,40960]{1,0,2:T(2,128)(2,1)} copy(bf16[2,16,40960]{2,1,0:T(8,128)(2,1)} %param.5) | data formatting | bytes 5242880 | tf_op args[0]
  38.6 24.1 %reshape.129 = bf16[8,2,81920]{2,1,0:T(2,128)(2,1)} reshape(bf16[40960,2,16]{2,1,0:T(2,128)(2,1)} %bitcast.40) | data formatting | bytes 5242880
  62.7 7.7 %all-to-all-start = ((bf16[8,2,81920]{2,1,0:T(2,128)(2,1)}), bf16[8,2,81920]{2,1,0:T(2,128)(2,1)S(1)}, u32[]{:S(2)}, u32[]{:S(2)}) async-start(bf16[8,2,81920]{2,1,0:T(2,128)(2,1)} %reshape.129), calls=%async_computation | async-start | bytes 5242880 | tf_op jit(solution)/shard_map/all_to_all | solution.py:37
  71.0 23.8 %copy.29 = bf16[160,8,2,5120]{3,1,2,0:T(8,128)(2,1)} copy(bf16[160,8,2,5120]{3,2,1,0:T(2,128)(2,1)} %bitcast.41) | data formatting | bytes 52428800
  94.8 35.0 %all-to-all-done = bf16[8,2,81920]{2,1,0:T(2,128)(2,1)S(1)} async-done(((bf16[8,2,81920]{2,1,0:T(2,128)(2,1)}), bf16[8,2,81920]{2,1,0:T(2,128)(2,1)S(1)}, u32[]{:S(2)}, u32[]{:S(2)}) %all-to-all-start) | async-done | bytes 2621472 | tf_op jit(solution)/shard_map/all_to_all | solution.py:37
  129.8 17.1 %reshape.130 = bf16[40960,2,16]{2,1,0:T(2,128)(2,1)} reshape(bf16[8,2,81920]{2,1,0:T(2,128)(2,1)S(1)} %all-to-all-done) | data formatting | bytes 5242880
  146.9 37.5 %copy.28 = bf16[2,16,8,5120]{3,1,2,0:T(8,128)(2,1)S(1)} copy(bf16[2,16,8,5120]{1,0,3,2:T(2,128)(2,1)} %bitcast.39) | data formatting | bytes 5242880 | tf_op jit(solution)/shard_map/all_to_all | solution.py:37
  184.4 0.3 bitcast_multiply_fusion
  184.7 0.2 slice_bitcast_fusion.1
  184.9 0.1 fusion.168
  185.0 27.8 %fusion.138 = f32[1280,256]{0,1:T(8,128)S(1)} fusion(bf16[1280,10240]{1,0:T(8,128)(2,1)} %bitcast.37, bf16[128,5120]{1,0:T(8,128)(2,1)S(1)} %fusion.168, bf16[128,5120]{1,0:T(8,128)(2,1)S(1)} %get-tuple-element.28, bf16[128,5120]{1,0:T(8,128)(2,1)S(1)} %get-tuple-element.27), kind=kOutput, calls=%fused_computation.122 | convolution fusion | flops 6731857920 | bytes 31457280 | tf_op jit(solution)/shard_map/dot_general | solution.py:53
  212.8 1.5 collective-permute-start
  214.3 28.1 %collective-permute-done = f32[1280,256]{0,1:T(8,128)S(1)} collective-permute-done((f32[1280,256]{0,1:T(8,128)S(1)}, f32[1280,256]{0,1:T(8,128)S(1)}, u32[]{:S(2)}, u32[]{:S(2)}) %collective-permute-start) | collective-permute-done | bytes 1310752 | tf_op jit(solution)/shard_map/ppermute | solution.py:12
  242.3 0.2 add.22
  242.5 0.0 copy-start.2
  242.5 0.0 copy-start.1
  242.6 0.8 collective-permute-start.1
  243.4 28.1 %collective-permute-done.1 = f32[1280,256]{0,1:T(8,128)S(1)} collective-permute-done((f32[1280,256]{0,1:T(8,128)S(1)}, f32[1280,256]{0,1:T(8,128)S(1)}, u32[]{:S(2)}, u32[]{:S(2)}) %collective-permute-start.1) | collective-permute-done | bytes 1310752 | tf_op jit(solution)/shard_map/ppermute | solution.py:12
  271.5 0.1 add.23
  271.6 3.3 collective-permute-start.2
  274.9 0.0 copy-done.2
  275.0 0.3 reduce-window.9
  275.3 0.1 slice.88
  275.4 0.1 slice_reduce_fusion.18
  275.5 0.0 copy-done.1
  275.5 0.3 slice_reduce_fusion.17
  275.7 0.1 add_bitcast_fusion
  275.8 0.3 select_reduce_fusion
  276.2 54.4 %collective-permute-done.2 = f32[1280,256]{0,1:T(8,128)S(1)} collective-permute-done((f32[1280,256]{0,1:T(8,128)S(1)}, f32[1280,256]{0,1:T(8,128)S(1)}, u32[]{:S(2)}, u32[]{:S(2)}) %collective-permute-start.2) | collective-permute-done | bytes 1310752 | tf_op jit(solution)/shard_map/ppermute | solution.py:12
  330.6 0.1 add.24
  330.7 0.0 copy-start
  330.7 1.0 copy-done
  331.8 37.9 %fusion = f32[1280,256]{1,0:T(8,128)} fusion(f32[1280,256]{0,1:T(8,128)S(1)} %add.24, f32[1280]{0:T(1024)S(1)} %get-tuple-element.19, f32[1280]{0:T(1024)S(1)} %get-tuple-element.20, f32[1280]{0:T(1024)S(1)} %get-tuple-element.4, f32[1280]{0:T(1024)S(1)} %get-tuple-element.5, f32[1280]{0:T(1024)S(1)} %get-tuple-element.6, f32[1280]{0:T(1024)S(1)} %get-tuple-element.7, ...), kind=kOutput, calls=%fused_computation | convolution fusion | flops 5123276800 | bytes 2741760 | tf_op jit(solution)/shard_map/dot_general | solution.py:59
  369.7 13.0 %fusion.144 = f32[256,10240]{1,0:T(8,128)S(1)} fusion(bf16[1280,10240]{1,0:T(8,128)(2,1)} %bitcast.38, f32[1280,256]{1,0:T(8,128)} %fusion), kind=kOutput, calls=%fused_computation.136 | convolution fusion | flops 6711214080 | bytes 38010880 | tf_op jit(solution)/shard_map/dot_general | solution.py:66
  382.7 0.8 fusion.142
  383.5 0.5 fusion.81
  383.9 4.2 copy.24
  388.1 4.9 %all-to-all-start.1 = ((bf16[2,128,5120]{2,0,1:T(2,128)(2,1)}), bf16[2,128,5120]{2,0,1:T(2,128)(2,1)S(1)}, u32[]{:S(2)}, u32[]{:S(2)}) async-start(bf16[2,128,5120]{2,0,1:T(2,128)(2,1)} %copy.24), calls=%async_computation.1 | async-start | bytes 5242880 | tf_op jit(solution)/shard_map/all_to_all | solution.py:74
  393.0 2.8 copy.26
  395.8 1.9 multiply_reduce_fusion
  397.7 0.6 fusion.169
  398.3 7.4 %psum.7 = f32[]{:T(128)} all-reduce(f32[]{:T(128)} %get-tuple-element.23), channel_id=1, replica_groups=mesh['ga'=8,'band'=4] {'band'}, use_global_device_ids=true, to_apply=%region_6.7 | all-reduce | flops 1 | bytes 8 | tf_op jit(solution)/shard_map/psum | solution.py:65
  405.7 0.6 dynamic_slice.3
  406.9 45.7 %all-to-all-done.1 = bf16[2,128,5120]{2,0,1:T(2,128)(2,1)S(1)} async-done(((bf16[2,128,5120]{2,0,1:T(2,128)(2,1)}), bf16[2,128,5120]{2,0,1:T(2,128)(2,1)S(1)}, u32[]{:S(2)}, u32[]{:S(2)}) %all-to-all-start.1) | async-done | bytes 2621472 | tf_op jit(solution)/shard_map/all_to_all | solution.py:74
  452.7 2.9 copy.25
  455.6 4.5 all_to_all.33
  (5 shorter events, 0.1 us)
Async XLA Ops:
  62.7 67.1 %all-to-all-start = ((bf16[8,2,81920]{2,1,0:T(2,128)(2,1)}), bf16[8,2,81920]{2,1,0:T(2,128)(2,1)S(1)}, u32[]{:S(2)}, u32[]{:S(2)}) async-start(bf16[8,2,81920]{2,1,0:T(2,128)(2,1)} %reshape.129), calls=%async_computation | async-start | bytes 5242880 | tf_op jit(solution)/shard_map/all_to_all | solution.py:37
  212.8 29.6 %collective-permute-start = (f32[1280,256]{0,1:T(8,128)S(1)}, f32[1280,256]{0,1:T(8,128)S(1)}, u32[]{:S(2)}, u32[]{:S(2)}) collective-permute-start(f32[1280,256]{0,1:T(8,128)S(1)} %fusion.138), channel_id=1, source_target_pairs={{0,4},{4,0},{8,12},{12,8},{16,20},{20,16},{24,28},{28,24},{1,5},{5... | collective-permute-start | bytes 3932168 | tf_op jit(solution)/shard_map/ppermute | solution.py:12
  242.5 32.4 %copy-start.2 = (s32[160]{0:T(256)S(1)}, s32[160]{0:T(256)}, u32[]{:S(2)}) copy-start(s32[160]{0:T(256)} %param.8) | copy-start | bytes 1924
  242.5 33.0 %copy-start.1 = (f32[1280,18]{0,1:T(8,128)S(1)}, f32[1280,18]{0,1:T(8,128)}, u32[]{:S(2)}) copy-start(f32[1280,18]{0,1:T(8,128)} %param.7) | copy-start | bytes 276484
  242.6 28.9 %collective-permute-start.1 = (f32[1280,256]{0,1:T(8,128)S(1)}, f32[1280,256]{0,1:T(8,128)S(1)}, u32[]{:S(2)}, u32[]{:S(2)}) collective-permute-start(f32[1280,256]{0,1:T(8,128)S(1)} %add.22), channel_id=1, source_target_pairs={{0,8},{4,12},{8,0},{12,4},{16,24},{20,28},{24,16},{28,20},{1,9},{5... | collective-permute-start | bytes 3932168 | tf_op jit(solution)/shard_map/ppermute | solution.py:12
  271.6 59.0 %collective-permute-start.2 = (f32[1280,256]{0,1:T(8,128)S(1)}, f32[1280,256]{0,1:T(8,128)S(1)}, u32[]{:S(2)}, u32[]{:S(2)}) collective-permute-start(f32[1280,256]{0,1:T(8,128)S(1)} %add.23), channel_id=1, source_target_pairs={{0,16},{4,20},{8,24},{12,28},{16,0},{20,4},{24,8},{28,12},{1,17},{... | collective-permute-start | bytes 3932168 | tf_op jit(solution)/shard_map/ppermute | solution.py:12
  330.7 1.1 copy-start
  388.1 64.5 %all-to-all-start.1 = ((bf16[2,128,5120]{2,0,1:T(2,128)(2,1)}), bf16[2,128,5120]{2,0,1:T(2,128)(2,1)S(1)}, u32[]{:S(2)}, u32[]{:S(2)}) async-start(bf16[2,128,5120]{2,0,1:T(2,128)(2,1)} %copy.24), calls=%async_computation.1 | async-start | bytes 5242880 | tf_op jit(solution)/shard_map/all_to_all | solution.py:74
